TPU v7x, 32 devices: a whole 2x2x4 slice. The times are simulated.
32 devices in a mesh: cls: 4 (over y, x), org: 8 (over z, core).
Axes of the slice: x: 2, y: 2, z: 4, core: 2. Of those that a mesh axis runs over, the one named last changes fastest.
Arguments:
- flows_start: float32 [8, 49152], P('cls', 'org'), may hold values from 150 to 300
- interaction: float32 [8, 8, 49152], P('cls', None, 'org'), may hold values from 0.2 to 2
- free_time: float32 [8, 49152], P('cls', 'org'), may hold values from 0.01 to 0.1
- capacity: float32 [49152], P('org'), may hold values from 300 to 900
- demand: int32 [8, 8, 60], P('cls', 'org'), may hold values from 0 to 15
- incidence: int32 [2, 8, 8, 2, 49152], P(None, 'cls', 'org'), may hold values from 0 to 1073741823, as said below
- step_size: float32 [2], replicated, may hold values from 0.3 to 0.6
Outputs:
- flows: float32 [8, 49152], P('cls', 'org')
- costs: float32 [8, 49152], P('cls', 'org')
- skims: float32 [2, 8, 8, 60], P(None, 'cls', 'org')
- gaps: float32 [2], replicated
Inputs may be any that keep to these rules, and one draw needn't show every extreme that they name: Bit b of incidence[k, c, o, w, l] tells whether link l lies on class c's path from anchor o to destination w * 30 + b in iteration k; each path is the union of 4 runs of 64 consecutive links (counted cyclically over the links) at drawn starts, the first of which is shared by all 30 destinations of one word.
All inputs are finite; a program needn't handle non-finite values.
Results may differ from a plain program's by a relative error of at most 0.0013.
Values sent between devices are 32-bit elements; how exact they have to be, the bound alone decides.
A program may use at most 256 MiB of HBM per device.

v0:
```python
import jax
import jax.numpy as jnp
from jax import lax
from jax.sharding import PartitionSpec as P

BITS = 30
ITERS = 2
HIGH = lax.Precision.HIGHEST


def unpack_half(packed):
    shifts = jnp.arange(BITS, dtype=jnp.int32)
    bit_table = jnp.bitwise_and(jnp.right_shift(packed[..., :, None, :], shifts[:, None]), 1)
    new_shape = packed.shape[:-2] + (packed.shape[-2] * BITS, packed.shape[-1])
    return bit_table.reshape(new_shape).astype(jnp.bfloat16)


def link_cost(flows_all, inter, free, cap):
    load_sum = jnp.einsum("cel,el->cl", inter, flows_all, precision=HIGH)
    load_ratio = load_sum / cap
    square = load_ratio * load_ratio
    return free * (1.0 + 0.15 * square * square)


def split_three(values):
    upper = values.astype(jnp.bfloat16)
    remain = values - upper.astype(jnp.float32)
    middle = remain.astype(jnp.bfloat16)
    lowest = (remain - middle.astype(jnp.float32)).astype(jnp.bfloat16)
    return jnp.stack([upper, middle, lowest], axis=1)


def skim_block(bit_table, cost_block):
    parts = split_three(cost_block)
    terms = jnp.einsum("codl,cpl->cpod", bit_table, parts, preferred_element_type=jnp.float32)
    return jnp.sum(terms, axis=1)


def anchor_loads_local(packed_all, trips_half, link_shard, block_count):

    def one_block(block_index):
        word_block = lax.dynamic_slice_in_dim(packed_all, block_index * link_shard, link_shard, 3)
        bit_table = unpack_half(word_block)
        return jnp.einsum("cod,codl->cl", trips_half, bit_table, preferred_element_type=jnp.float32)

    blocks = lax.map(one_block, jnp.arange(block_count, dtype=jnp.int32))
    return jnp.moveaxis(blocks, 0, 1).reshape(blocks.shape[1], block_count * link_shard)


def make_fold(packed_all, link_shard):

    def fold_links(skim_carry, portion, first):
        turn_count = portion.shape[1] // link_shard

        def advance(skim_sum, block_index):
            offset = block_index * link_shard
            word_block = lax.dynamic_slice_in_dim(packed_all, offset, link_shard, 3)
            bit_table = unpack_half(word_block)
            cost_block = lax.dynamic_slice_in_dim(portion, offset, link_shard, 1)
            return (skim_sum + skim_block(bit_table, cost_block), None)

        result, unused = lax.scan(advance, skim_carry, jnp.arange(turn_count, dtype=jnp.int32))
        return result

    return fold_links


def both_totals(cost_part, path_part):
    return lax.psum((cost_part, path_part), ("cls", "org"))


def shards(flows_start, interaction, free_time, capacity, demand, incidence, step_size):
    org_count = lax.axis_size("org")
    link_shard = flows_start.shape[1]
    dest_count = demand.shape[2]
    class_local = demand.shape[0]
    demand_real = demand.astype(jnp.float32)
    trips_half = demand.astype(jnp.bfloat16)
    own_start = lax.axis_index("org") * link_shard
    skim_init = jnp.zeros((class_local, demand.shape[1], dest_count), jnp.float32)
    skim_list = []
    gap_list = []
    inter_full, free_full, cap_full, flow_now = (
        lax.all_gather(interaction, "org", axis=2, tiled=True),
        lax.all_gather(free_time, "org", axis=1, tiled=True),
        lax.all_gather(capacity, "org", axis=0, tiled=True),
        lax.all_gather(flows_start, "org", axis=1, tiled=True),
    )

    def full_cost(flow_value):
        flows_all = lax.all_gather(flow_value, "cls", axis=0, tiled=True)
        return link_cost(flows_all, inter_full, free_full, cap_full)

    for iteration in range(ITERS):
        cost_now = full_cost(flow_now)
        fold_links = make_fold(incidence[iteration], link_shard)
        skim_now = fold_links(skim_init, cost_now, jnp.int32(0))
        partial_value = anchor_loads_local(incidence[iteration], trips_half, link_shard, org_count)
        aon = lax.psum(partial_value, "org")
        product = lax.dynamic_slice_in_dim(cost_now * flow_now, own_start, link_shard, 1)
        cost_total, path_total = both_totals(jnp.sum(product), jnp.sum(demand_real * skim_now))
        gap_list.append((cost_total - path_total) / cost_total)
        skim_list.append(skim_now)
        flow_now = flow_now + step_size[iteration] * (aon - flow_now)
    cost_final = full_cost(flow_now)
    flow_out = lax.dynamic_slice_in_dim(flow_now, own_start, link_shard, 1)
    cost_out = lax.dynamic_slice_in_dim(cost_final, own_start, link_shard, 1)
    return (flow_out, cost_out, jnp.stack(skim_list), jnp.stack(gap_list))


def solution(mesh):
    placed = (
        P("cls", "org"),
        P("cls", None, "org"),
        P("cls", "org"),
        P("org"),
        P("cls", "org", None),
        P(None, "cls", "org", None, None),
        P(),
    )
    return jax.shard_map(
        shards,
        mesh=mesh,
        in_specs=placed,
        out_specs=(P("cls", "org"), P("cls", "org"), P(None, "cls", "org", None), P()),
        check_vma=False,
    )
```

profile of v0, /device:TPU:0, one launch (start us, length us, event | category | flops | bytes accessed | tf_op | source)
XLA Modules:
  0.0 387.4 jit_solution(10713880894416797273)
XLA Ops:
  10.9 32.3 %while.43 = (s32[]{:T(128)}, f32[8,2,6144]{2,1,0:T(2,128)S(1)}, s32[8]{0:T(128)S(1)}, s32[2,1,2,49152]{3,0,2,1:T(2,128)S(1)}, bf16[2,1,60]{2,0,1:T(2,128)(2,1)S(...) while((s32[]{:T(128)}, f32[8,2,6144]{2,1,0:T(2,128)S(1)}, s32[8]{0:T(128)S(1)}, ...), condition=%wide.region_4.5_spmd, body=%wide.region_3.4_spmd.sunk | while | flops 3686406 | bytes 3392847 | solution.py:46
  12.3 1.7 fusion.83
  16.3 1.7 fusion.83
  28.4 1.7 fusion.83
  32.5 1.7 fusion.83
  36.5 1.7 fusion.83
  40.5 1.7 fusion.83
  44.3 32.3 %while.42 = (s32[]{:T(128)}, f32[8,2,6144]{2,1,0:T(2,128)S(1)}, s32[8]{0:T(128)S(1)}, s32[2,1,2,49152]{3,0,2,1:T(2,128)S(1)}, bf16[2,1,60]{2,0,1:T(2,128)(2,1)S(...) while((s32[]{:T(128)}, f32[8,2,6144]{2,1,0:T(2,128)S(1)}, s32[8]{0:T(128)S(1)}, ...), condition=%wide.region_1.0_spmd, body=%wide.region_0.1_spmd.sunk | while | flops 3686406 | bytes 3392847 | solution.py:46
  53.8 1.7 fusion.79
  57.8 1.7 fusion.79
  77.5 17.5 %all_gather.21 = f32[2,49152]{1,0:T(2,128)} all-gather(f32[2,6144]{1,0:T(2,128)S(1)} %copy-done.7), channel_id=1, replica_groups=mesh['cls'=4,'org'=8] {'org'}, dimensions={1}, use_global_device_ids=true | all-gather | bytes 442368 | tf_op jit(solution)/shard_map/all_gather | solution.py:87
  95.7 42.7 %all-reduce.4.cloned.1.call-done = (f32[2,49152]{1,0:T(2,128)}, f32[2,49152]{1,0:T(2,128)}) async-done(((f32[2,49152]{1,0:T(2,128)}, f32[2,49152]{1,0:T(2,128)}), (f32[2,49152]{1,0:T(2,128)}, f32[2,49152]{1,0:T(2,128)})) %all-reduce.4.cloned.1.call-update) | async-done | bytes 786448 | tf_op jit(solution)/shard_map/psum | solution.py:99
  138.4 3.8 multiply_add_fusion
  143.5 15.2 %all_gather.25 = f32[49152]{0:T(1024)} all-gather(f32[6144]{0:T(1024)S(1)} %copy-done.9), channel_id=1, replica_groups=mesh['cls'=4,'org'=8] {'org'}, dimensions={0}, use_global_device_ids=true | all-gather | bytes 221184 | tf_op jit(solution)/shard_map/all_gather | solution.py:86
  158.7 14.7 %all_gather.22 = f32[2,49152]{1,0:T(2,128)S(1)} all-gather(f32[2,6144]{1,0:T(2,128)S(1)} %copy-done.8), channel_id=1, replica_groups=mesh['cls'=4,'org'=8] {'org'}, dimensions={1}, use_global_device_ids=true | all-gather | bytes 442368 | tf_op jit(solution)/shard_map/all_gather | solution.py:85
  174.8 2.5 reshape.94
  177.3 2.5 reshape.92
  179.8 24.8 %all-gather.14.cloned.1.call-done = f32[4,2,49152]{2,1,0:T(2,128)} async-done(((f32[1,2,49152]{2,1,0:T(2,128)}), f32[4,2,49152]{2,1,0:T(2,128)}) %all-gather.14.cloned.1.call-update) | async-done | bytes 1572880 | tf_op jit(solution)/shard_map/all_gather | solution.py:91
  204.6 3.6 reshape.96
  208.2 36.0 %all-gather.8.cloned.1.call-done = f32[2,8,49152]{2,1,0:T(8,128)} async-done(((f32[2,8,6144]{2,1,0:T(8,128)}), f32[2,8,49152]{2,1,0:T(8,128)}) %all-gather.8.cloned.1.call-update) | async-done | bytes 3145744 | tf_op jit(solution)/shard_map/all_gather | solution.py:84
  244.2 6.9 %multiply_reduce_fusion.1 = (f32[49152,2]{0,1:T(2,128)S(1)}, f32[49152,2]{0,1:T(2,128)S(1)}, f32[49152,2]{0,1:T(2,128)}) fusion(f32[2,8,49152]{2,1,0:T(8,128)} %all-gather.8.cloned.1.call-done, f32[49152,8]{0,1:T(8,128)S(1)} %bitcast.155, f32[49152,8]{0,1:T(8,128)} %bitcast.157, f32[49152,8]{0,1:T(8,128)S(1)} %bitcast.156), kind=kLoop, calls=%fused_computation.59 | loop fusion | flops 4423680 | bytes 9043968 | tf_op jit(solution)/shard_map/cel,el->cl/dot_general | solution.py:19
  253.4 39.4 %while.44 = (s32[]{:T(128)}, f32[2,1,60]{2,0,1:T(2,128)S(1)}, s32[8]{0:T(128)S(1)}, f32[2,49152]{1,0:T(2,128)S(1)}, s32[2,1,2,49152]{3,0,2,1:T(2,128)}, /*index=5*/s32[]{:T(128)}, s32[1]{0:T(128)}, s32[]{:T(128)}, s32[]{:T(128)}) while((s32[]{:T(128)}, f32[2,1,60]{2,0,1:T(2,128)S(1)}, s32[8]{0:T(128)S(1)}, ...), condition=%wide.region_8.9_spmd.clone, body=%wide.region_6.8_spmd.clone.sunk | while | flops 6943207 | bytes 3615725 | solution.py:62
  294.2 39.4 %while.45 = (s32[]{:T(128)}, f32[2,1,60]{2,0,1:T(2,128)S(1)}, s32[8]{0:T(128)S(1)}, f32[2,49152]{1,0:T(2,128)S(1)}, s32[2,1,2,49152]{3,0,2,1:T(2,128)}, /*index=5*/s32[]{:T(128)}, s32[1]{0:T(128)}, s32[]{:T(128)}, s32[]{:T(128)}) while((s32[]{:T(128)}, f32[2,1,60]{2,0,1:T(2,128)S(1)}, s32[8]{0:T(128)S(1)}, ...), condition=%wide.region_11.12_spmd.clone, body=%wide.region_9.11_spmd.clone.sunk | while | flops 6943207 | bytes 3615725 | solution.py:62
  334.2 39.7 %all-reduce = (f32[]{:T(128)}, f32[]{:T(128)}, f32[]{:T(128)}, f32[]{:T(128)}) all-reduce(f32[]{:T(128)} %fusion.53, f32[]{:T(128)} %get-tuple-element.186, f32[]{:T(128)} %fusion.54, f32[]{:T(128)} %get-tuple-element.185), channel_id=1, replica_groups=mesh['cls'=4,'org'=8] {'cls','org'}, use_global_device_ids=true, to_apply=%region_17.18 | all-reduce | flops 4 | bytes 32 | tf_op jit(solution)/shard_map/psum | solution.py:69
  (353 shorter events, 121.2 us)
Async XLA Ops:
  8.0 130.4 %all-reduce.4.cloned.1.call-start = ((), (), s32[]{:S(2)}) async-start(), calls=%async_computation.4 | async-start | bytes 1572864 | tf_op jit(solution)/shard_map/psum | solution.py:99
  8.0 1.5 copy-start.11
  43.2 1.0 copy-start
  43.2 1.1 copy-start.6
  43.3 34.1 %copy-start.7 = (f32[2,6144]{1,0:T(2,128)S(1)}, f32[2,6144]{1,0:T(2,128)}, u32[]{:S(2)}) copy-start(f32[2,6144]{1,0:T(2,128)} %param.15) | copy-start | bytes 147460
  76.6 0.8 copy-start.5
  76.6 65.5 %copy-start.1 = (s32[2,1,2,49152]{3,0,2,1:T(2,128)}, s32[2,1,2,49152]{3,0,2,1:T(2,128)S(1)}, u32[]{:S(2)}) copy-start(s32[2,1,2,49152]{3,0,2,1:T(2,128)S(1)} %get-tuple-element.496) | copy-start | bytes 2359300
  76.6 18.4 %copy-start.10 = (f32[2]{0:T(128)S(1)}, f32[2]{0:T(128)}, u32[]{:S(2)}) copy-start(f32[2]{0:T(128)} %param.21) | copy-start | bytes 28
  77.4 97.4 %all-gather.12.cloned.1.call-start = ((), (), s32[]{:S(2)}) async-start(), calls=%async_computation.2 | async-start | bytes 1966080 | tf_op jit(solution)/shard_map/all_gather | solution.py:91
  95.0 82.3 %all-gather.10.cloned.1.call-start = ((), (), s32[]{:S(2)}) async-start(), calls=%async_computation.1 | async-start | bytes 1966080 | tf_op jit(solution)/shard_map/all_gather | solution.py:91
  138.4 5.1 %copy-start.9 = (f32[6144]{0:T(1024)S(1)}, f32[6144]{0:T(1024)}, u32[]{:S(2)}) copy-start(f32[6144]{0:T(1024)} %param.18) | copy-start | bytes 73732
  138.4 20.3 %copy-start.8 = (f32[2,6144]{1,0:T(2,128)S(1)}, f32[2,6144]{1,0:T(2,128)}, u32[]{:S(2)}) copy-start(f32[2,6144]{1,0:T(2,128)} %param.17) | copy-start | bytes 147460
  142.2 62.4 %all-gather.14.cloned.1.call-start = ((), (), s32[]{:S(2)}) async-start(), calls=%async_computation.3 | async-start | bytes 1966080 | tf_op jit(solution)/shard_map/all_gather | solution.py:91
  142.8 101.5 %all-gather.8.cloned.1.call-start = ((), (), s32[]{:S(2)}) async-start(), calls=%async_computation | async-start | bytes 3538944 | tf_op jit(solution)/shard_map/all_gather | solution.py:84
  244.2 6.9 %copy-start.2 = (f32[49152]{0:T(1024)S(1)}, f32[49152]{0:T(1024)}, u32[]{:S(2)}) copy-start(f32[49152]{0:T(1024)} %all_gather.25) | copy-start | bytes 589828
  294.2 83.5 %copy-start.3 = (f32[49152]{0:T(1024)S(1)}, f32[49152]{0:T(1024)}, u32[]{:S(2)}) copy-start(f32[49152]{0:T(1024)} %all_gather.25) | copy-start | bytes 589828
  294.2 83.5 %copy-start.4 = (f32[49152,2]{0,1:T(2,128)S(1)}, f32[49152,2]{0,1:T(2,128)}, u32[]{:S(2)}) copy-start(f32[49152,2]{0,1:T(2,128)} %get-tuple-element.184) | copy-start | bytes 1179652
Sparse Core Ops, SparseCore 0:
  77.5 60.7 all-reduce.3
Sparse Core Ops, SparseCore 1:
  95.1 31.7 all-gather.11
  142.3 29.8 all-gather.9
  173.8 30.7 all-gather.13
  206.2 38.0 all-gather.7
where the time goes:
time: 389 us; the launch traced here: 387 us
  waiting for transfers between devices  105 us (27%)
  blocking collectives  87 us (22%)
  other arithmetic  73.1 us (19%)
  local copies, waits for them, and re-layouts  54.4 us (14%)
  matrix products  25.3 us (7%)
  loops' own time  22.7 us (6%)
  between operations  19.7 us (5%)
    convert_element_type x32, other arithmetic, unpack_half(): return bit_table.reshape(new_shape).astype(jnp.bfloat16)  55.2 us
    psum x1, waiting for transfers between devices, shards(): aon = lax.psum(partial_value, 'org')  42.7 us
    psum x1, blocking collectives, both_totals(): return lax.psum((cost_part, path_part), ('cls', 'org'))  39.7 us
    all_gather x1, waiting for transfers between devices, shards(): lax.all_gather(interaction, 'org', axis=2, tiled=True)  36 us
    all_gather x3, waiting for transfers between devices, full_cost(): flows_all = lax.all_gather(flow_value, 'cls', axis=0, tiled=True)  24.8 us
    dynamic_slice x32, local copies, waits for them, and re-layouts, fold_links(): lax.scan(advance, skim_carry, jnp.arange(turn_count, dtype=jnp.int32))  18.8 us
    all_gather x1, blocking collectives, shards(): lax.all_gather(flows_start, 'org', axis=1, tiled=True)  17.5 us
    shift_right_arithmetic x96, local copies, waits for them, and re-layouts, unpack_half(): jnp.right_shift(packed[..., :, None, :], shifts[:, None])  17.5 us
  transfers between devices with their start and end apart: 5, of which 3 were waited for; matrix products, arithmetic and copies ran while one was open for 4% of the time, Pallas kernels for 0%

commit v1 on v0

--- a/solution.py
+++ b/solution.py
@@ -96,7 +96,7 @@
         fold_links = make_fold(incidence[iteration], link_shard)
         skim_now = fold_links(skim_init, cost_now, jnp.int32(0))
         partial_value = anchor_loads_local(incidence[iteration], trips_half, link_shard, org_count)
-        aon = lax.psum(partial_value, "org")
+        aon = jnp.sum(lax.all_gather(partial_value, "org"), axis=0)
         product = lax.dynamic_slice_in_dim(cost_now * flow_now, own_start, link_shard, 1)
         cost_total, path_total = both_totals(jnp.sum(product), jnp.sum(demand_real * skim_now))
         gap_list.append((cost_total - path_total) / cost_total)

time: 389 us -> 403 us (1.036)
  waiting for transfers between devices: 105 us -> 115 us
  other arithmetic: 73.1 us -> 78 us
    psum x1 -> x0, waiting for transfers between devices: 42.7 us -> none  [shards(): aon = lax.psum(partial_value, 'org')]
    all_gather x3, waiting for transfers between devices: 24.8 us -> 52.6 us  [full_cost(): flows_all = lax.all_gather(flow_value, 'cls', axis=0, tiled=True)]
    all_gather x0 -> x2, waiting for transfers between devices: none -> 25.3 us  [shards(): aon = jnp.sum(lax.all_gather(partial_value, 'org'), axis=0)]
    reduce_sum x0 -> x2, other arithmetic: none -> 6.09 us  [shards(): aon = jnp.sum(lax.all_gather(partial_value, 'org'), axis=0)]
    unnamed x27 -> x31, local copies, waits for them, and re-layouts: 10.4 us -> 10.3 us
  transfers between devices with their start and end apart: 5 -> 6, of which waited for: 3 -> 4; matrix products, arithmetic and copies ran while one was open for 4% -> 11% of each run, Pallas kernels for 0% -> 0%
where the time goes in v1:
time: 403 us; the launch traced here: 402 us
  waiting for transfers between devices  115 us (29%)
  blocking collectives  87.7 us (22%)
  other arithmetic  78 us (19%)
  local copies, waits for them, and re-layouts  54.4 us (13%)
  matrix products  25.3 us (6%)
  loops' own time  22.7 us (6%)
  between operations  18.2 us (5%)
    convert_element_type x32, other arithmetic, unpack_half(): return bit_table.reshape(new_shape).astype(jnp.bfloat16)  55.2 us
    all_gather x3, waiting for transfers between devices, full_cost(): flows_all = lax.all_gather(flow_value, 'cls', axis=0, tiled=True)  52.6 us
    psum x1, blocking collectives, both_totals(): return lax.psum((cost_part, path_part), ('cls', 'org'))  39.6 us
    all_gather x1, waiting for transfers between devices, shards(): lax.all_gather(interaction, 'org', axis=2, tiled=True)  36 us
    all_gather x2, waiting for transfers between devices, shards(): aon = jnp.sum(lax.all_gather(partial_value, 'org'), axis=0)  25.3 us
    dynamic_slice x32, local copies, waits for them, and re-layouts, fold_links(): lax.scan(advance, skim_carry, jnp.arange(turn_count, dtype=jnp.int32))  18.8 us
    shift_right_arithmetic x96, local copies, waits for them, and re-layouts, unpack_half(): jnp.right_shift(packed[..., :, None, :], shifts[:, None])  17.5 us
    all_gather x1, blocking collectives, shards(): lax.all_gather(flows_start, 'org', axis=1, tiled=True)  17.3 us
  transfers between devices with their start and end apart: 6, of which 4 were waited for; matrix products, arithmetic and copies ran while one was open for 11% of the time, Pallas kernels for 0%

profile of v1, /device:TPU:0, one launch (start us, length us, event | category | flops | bytes accessed | tf_op | source)
XLA Modules:
  0.0 401.7 jit_solution(4225735668020664349)
XLA Ops:
  10.1 32.3 %while.42 = (s32[]{:T(128)}, f32[8,2,6144]{2,1,0:T(2,128)S(1)}, s32[8]{0:T(128)S(1)}, s32[2,1,2,49152]{3,0,2,1:T(2,128)S(1)}, bf16[2,1,60]{2,0,1:T(2,128)(2,1)S(...) while((s32[]{:T(128)}, f32[8,2,6144]{2,1,0:T(2,128)S(1)}, s32[8]{0:T(128)S(1)}, ...), condition=%wide.region_1.0_spmd, body=%wide.region_0.1_spmd.sunk | while | flops 3686406 | bytes 3392847 | solution.py:46
  11.4 1.7 fusion.79
  15.5 1.7 fusion.79
  19.5 1.7 fusion.79
  23.6 1.7 fusion.79
  43.5 32.3 %while.43 = (s32[]{:T(128)}, f32[8,2,6144]{2,1,0:T(2,128)S(1)}, s32[8]{0:T(128)S(1)}, s32[2,1,2,49152]{3,0,2,1:T(2,128)S(1)}, bf16[2,1,60]{2,0,1:T(2,128)(2,1)S(...) while((s32[]{:T(128)}, f32[8,2,6144]{2,1,0:T(2,128)S(1)}, s32[8]{0:T(128)S(1)}, ...), condition=%wide.region_4.5_spmd, body=%wide.region_3.4_spmd.sunk | while | flops 3686406 | bytes 3392847 | solution.py:46
  48.9 1.7 fusion.83
  76.7 17.3 %all_gather.27 = f32[2,49152]{1,0:T(2,128)} all-gather(f32[2,6144]{1,0:T(2,128)S(1)} %copy-done.9), channel_id=1, replica_groups=mesh['cls'=4,'org'=8] {'org'}, dimensions={1}, use_global_device_ids=true | all-gather | bytes 442368 | tf_op jit(solution)/shard_map/all_gather | solution.py:87
  94.6 3.0 reduce_sum.76
  97.7 25.3 %all-gather.12.cloned.1.call-done = f32[8,2,49152]{2,1,0:T(2,128)} async-done(((f32[1,2,49152]{2,1,0:T(2,128)}), f32[8,2,49152]{2,1,0:T(2,128)}) %all-gather.12.cloned.1.call-update) | async-done | bytes 3145744 | tf_op jit(solution)/shard_map/all_gather | solution.py:99
  123.0 3.0 reduce_sum.77
  126.1 2.6 multiply_add_fusion
  129.9 15.2 %all_gather.33 = f32[49152]{0:T(1024)} all-gather(f32[6144]{0:T(1024)S(1)} %copy-done.11), channel_id=1, replica_groups=mesh['cls'=4,'org'=8] {'org'}, dimensions={0}, use_global_device_ids=true | all-gather | bytes 221184 | tf_op jit(solution)/shard_map/all_gather | solution.py:86
  145.1 15.7 %all_gather.30 = f32[2,49152]{1,0:T(2,128)} all-gather(f32[2,6144]{1,0:T(2,128)S(1)} %copy-done.10), channel_id=1, replica_groups=mesh['cls'=4,'org'=8] {'org'}, dimensions={1}, use_global_device_ids=true | all-gather | bytes 442368 | tf_op jit(solution)/shard_map/all_gather | solution.py:85
  160.7 2.5 reshape.86
  164.7 22.6 %all-gather.16.cloned.1.call-done = f32[4,2,49152]{2,1,0:T(2,128)} async-done(((f32[1,2,49152]{2,1,0:T(2,128)}), f32[4,2,49152]{2,1,0:T(2,128)}) %all-gather.16.cloned.1.call-update) | async-done | bytes 1572880 | tf_op jit(solution)/shard_map/all_gather | solution.py:91
  187.2 2.5 reshape.84
  189.7 30.1 %all-gather.20.cloned.1.call-done = f32[4,2,49152]{2,1,0:T(2,128)} async-done(((f32[1,2,49152]{2,1,0:T(2,128)}), f32[4,2,49152]{2,1,0:T(2,128)}) %all-gather.20.cloned.1.call-update) | async-done | bytes 1572880 | tf_op jit(solution)/shard_map/all_gather | solution.py:91
  219.8 3.7 reshape.88
  223.4 36.0 %all-gather.14.cloned.1.call-done = f32[2,8,49152]{2,1,0:T(8,128)} async-done(((f32[2,8,6144]{2,1,0:T(8,128)}), f32[2,8,49152]{2,1,0:T(8,128)}) %all-gather.14.cloned.1.call-update) | async-done | bytes 3145744 | tf_op jit(solution)/shard_map/all_gather | solution.py:84
  259.5 6.9 %multiply_reduce_fusion.1 = (f32[49152,2]{0,1:T(2,128)S(1)}, f32[49152,2]{0,1:T(2,128)S(1)}, f32[49152,2]{0,1:T(2,128)}) fusion(f32[2,8,49152]{2,1,0:T(8,128)} %all-gather.14.cloned.1.call-done, f32[49152,8]{0,1:T(8,128)S(1)} %bitcast.155, f32[49152,8]{0,1:T(8,128)} %bitcast.157, f32[49152,8]{0,1:T(8,128)S(1)} %bitcast.156), kind=kLoop, calls=%fused_computation.59 | loop fusion | flops 4423680 | bytes 9043968 | tf_op jit(solution)/shard_map/cel,el->cl/dot_general | solution.py:19
  267.8 39.4 %while.44 = (s32[]{:T(128)}, f32[2,1,60]{2,0,1:T(2,128)S(1)}, s32[8]{0:T(128)S(1)}, f32[2,49152]{1,0:T(2,128)S(1)}, s32[2,1,2,49152]{3,0,2,1:T(2,128)}, /*index=5*/s32[]{:T(128)}, s32[1]{0:T(128)}, s32[]{:T(128)}, s32[]{:T(128)}) while((s32[]{:T(128)}, f32[2,1,60]{2,0,1:T(2,128)S(1)}, s32[8]{0:T(128)S(1)}, ...), condition=%wide.region_8.9_spmd.clone, body=%wide.region_6.8_spmd.clone.sunk | while | flops 6943207 | bytes 3615725 | solution.py:62
  308.7 39.4 %while.45 = (s32[]{:T(128)}, f32[2,1,60]{2,0,1:T(2,128)S(1)}, s32[8]{0:T(128)S(1)}, f32[2,49152]{1,0:T(2,128)S(1)}, s32[2,1,2,49152]{3,0,2,1:T(2,128)}, /*index=5*/s32[]{:T(128)}, s32[1]{0:T(128)}, s32[]{:T(128)}, s32[]{:T(128)}) while((s32[]{:T(128)}, f32[2,1,60]{2,0,1:T(2,128)S(1)}, s32[8]{0:T(128)S(1)}, ...), condition=%wide.region_11.12_spmd.clone, body=%wide.region_9.11_spmd.clone.sunk | while | flops 6943207 | bytes 3615725 | solution.py:62
  348.6 39.6 %all-reduce = (f32[]{:T(128)}, f32[]{:T(128)}, f32[]{:T(128)}, f32[]{:T(128)}) all-reduce(f32[]{:T(128)} %fusion.53, f32[]{:T(128)} %get-tuple-element.186, f32[]{:T(128)} %fusion.54, f32[]{:T(128)} %get-tuple-element.185), channel_id=1, replica_groups=mesh['cls'=4,'org'=8] {'cls','org'}, use_global_device_ids=true, to_apply=%region_17.18 | all-reduce | flops 4 | bytes 32 | tf_op jit(solution)/shard_map/psum | solution.py:69
  (362 shorter events, 126.2 us)
Async XLA Ops:
  7.2 1.5 copy-start.13
  7.2 87.4 %all-gather.10.cloned.1.call-start = ((), (), s32[]{:S(2)}) async-start(), calls=%async_computation | async-start | bytes 3538944 | tf_op jit(solution)/shard_map/all_gather | solution.py:99
  42.4 0.7 copy-start.7
  42.4 1.1 copy-start.1
  43.1 79.9 %all-gather.12.cloned.1.call-start = ((), (), s32[]{:S(2)}) async-start(), calls=%async_computation.1 | async-start | bytes 3538944 | tf_op jit(solution)/shard_map/all_gather | solution.py:99
  43.3 33.3 %copy-start.9 = (f32[2,6144]{1,0:T(2,128)S(1)}, f32[2,6144]{1,0:T(2,128)}, u32[]{:S(2)}) copy-start(f32[2,6144]{1,0:T(2,128)} %param.15) | copy-start | bytes 147460
  43.3 50.7 %copy-start.12 = (f32[2]{0:T(128)S(1)}, f32[2]{0:T(128)}, u32[]{:S(2)}) copy-start(f32[2]{0:T(128)} %param.21) | copy-start | bytes 28
  75.8 0.8 copy-start.8
  75.8 21.8 %copy-start = (s32[2,1,2,49152]{3,0,2,1:T(2,128)}, s32[2,1,2,49152]{3,0,2,1:T(2,128)S(1)}, u32[]{:S(2)}) copy-start(s32[2,1,2,49152]{3,0,2,1:T(2,128)S(1)} %get-tuple-element.491) | copy-start | bytes 2359300
  76.6 84.2 %all-gather.18.cloned.1.call-start = ((), (), s32[]{:S(2)}) async-start(), calls=%async_computation.4 | async-start | bytes 1966080 | tf_op jit(solution)/shard_map/all_gather | solution.py:91
  94.0 93.2 %all-gather.16.cloned.1.call-start = ((), (), s32[]{:S(2)}) async-start(), calls=%async_computation.3 | async-start | bytes 1966080 | tf_op jit(solution)/shard_map/all_gather | solution.py:91
  97.7 28.4 %copy-start.2 = (f32[2,49152]{1,0:T(2,128)S(1)}, f32[2,49152]{1,0:T(2,128)}, u32[]{:S(2)}) copy-start(f32[2,49152]{1,0:T(2,128)} %all_gather.27) | copy-start | bytes 1179652
  126.1 3.8 copy-start.11
  126.1 19.0 %copy-start.10 = (f32[2,6144]{1,0:T(2,128)S(1)}, f32[2,6144]{1,0:T(2,128)}, u32[]{:S(2)}) copy-start(f32[2,6144]{1,0:T(2,128)} %param.17) | copy-start | bytes 147460
  128.7 91.1 %all-gather.20.cloned.1.call-start = ((), (), s32[]{:S(2)}) async-start(), calls=%async_computation.5 | async-start | bytes 1966080 | tf_op jit(solution)/shard_map/all_gather | solution.py:91
  129.3 130.2 %all-gather.14.cloned.1.call-start = ((), (), s32[]{:S(2)}) async-start(), calls=%async_computation.2 | async-start | bytes 3538944 | tf_op jit(solution)/shard_map/all_gather | solution.py:84
  259.5 6.9 %copy-start.3 = (f32[2,49152]{1,0:T(2,128)S(1)}, f32[2,49152]{1,0:T(2,128)}, u32[]{:S(2)}) copy-start(f32[2,49152]{1,0:T(2,128)} %all_gather.30) | copy-start | bytes 1179652
  259.5 6.9 %copy-start.4 = (f32[49152]{0:T(1024)S(1)}, f32[49152]{0:T(1024)}, u32[]{:S(2)}) copy-start(f32[49152]{0:T(1024)} %all_gather.33) | copy-start | bytes 589828
  308.6 83.4 %copy-start.5 = (f32[49152]{0:T(1024)S(1)}, f32[49152]{0:T(1024)}, u32[]{:S(2)}) copy-start(f32[49152]{0:T(1024)} %all_gather.33) | copy-start | bytes 589828
  308.6 83.4 %copy-start.6 = (f32[49152,2]{0,1:T(2,128)S(1)}, f32[49152,2]{0,1:T(2,128)}, u32[]{:S(2)}) copy-start(f32[49152,2]{0,1:T(2,128)} %get-tuple-element.184) | copy-start | bytes 1179652
Sparse Core Ops, SparseCore 0:
  43.3 40.9 all-gather.9
  85.9 37.0 all-gather.11
  124.9 29.7 all-gather.17
  156.3 30.8 all-gather.15
  188.9 30.8 all-gather.19
  221.2 38.1 all-gather.13
